TPU v7x, 256 devices: a whole 4x4x8 slice. The times are simulated.
256 devices in a mesh: cfg: 2 (over y_hi), seq: 16 (over z, core), tp: 8 (over y_lo, x).
Axes of the slice: x: 4, y: 4 (y_hi: 2, y_lo: 2; y = y_hi * 2 + y_lo), z: 8, core: 2. Of those that a mesh axis runs over, the one named last changes fastest.
Arguments:
- queries: bfloat16 [2, 7680, 5120], P('cfg', 'seq', 'tp'), may hold values from -5 to 5
- keys: bfloat16 [2, 7680, 5120], P('cfg', 'seq', 'tp'), may hold values from -5 to 5
- values: bfloat16 [2, 7680, 5120], P('cfg', 'seq', 'tp'), may hold values from -5 to 5
- text_keys: bfloat16 [2, 512, 5120], P('cfg', None, 'tp'), may hold values from -7.5 to 7.5
- text_values: bfloat16 [2, 512, 5120], P('cfg', None, 'tp'), may hold values from -5 to 5
- prompt_lengths: int32 [2], P('cfg'), may hold values from 64 to 512
- frame_counts: int32 [16], P('seq'), may hold values from 240 to 480
- out_weight: bfloat16 [5120, 5120], P('tp'), may hold values from -0.5 to 0.5
Outputs:
- velocity: bfloat16 [7680, 5120], P('seq', ('tp', 'cfg'))
All inputs are finite; a program needn't handle non-finite values.
Results may differ from a plain program's by a relative error of at most 0.015.
Values may be sent and summed in bfloat16 or wider, within the bound.
A program may use at most 256 MiB of HBM per device.

v0:
```python
import jax
import jax.numpy as jnp
from jax import lax
from jax.sharding import PartitionSpec as P

HEAD_DIM = 128
FRAME_SLOTS = 480
GUIDANCE = 5.0
RESCALE = 0.7
NEGATIVE = -1e30


def in_order(pieces, dim):
    dims = list(pieces.shape[1:])
    dims[dim] *= pieces.shape[0]
    return jnp.moveaxis(pieces, 0, dim).reshape(dims)


def from_everyone(value, axis):
    devices = lax.axis_size(axis)
    return lax.all_to_all(
        jnp.broadcast_to(value[None], (devices, *value.shape)), axis, 0, 0, tiled=True
    )


def gathered_copies(value, axis, dim):
    return in_order(from_everyone(value, axis), dim)


def of_everyone(value, axis):
    return from_everyone(value, axis).sum(axis=0)


def together(arrays, axis):
    ends = [0]
    for a in arrays:
        ends.append(ends[-1] + a.size)
    running = of_everyone(jnp.concatenate([a.ravel() for a in arrays]), axis)
    return tuple((running[b:e].reshape(a.shape) for a, b, e in zip(arrays, ends, ends[1:])))


def frame_valid(positions, counts_table):
    frame_index = positions // FRAME_SLOTS
    slot_index = positions % FRAME_SLOTS
    frame_ids = jnp.arange(counts_table.shape[0], dtype=jnp.int32)
    frame_limit = jnp.sum(
        jnp.where(frame_index[:, None] == frame_ids[None, :], counts_table[None, :], 0), axis=1
    )
    return slot_index < frame_limit


def attend_block(carry, key_rows, value_rows, query_heads, key_mask):
    row_max, weight_sum, mixed_sum = carry
    head_count = query_heads.shape[1]
    key_heads = key_rows.reshape(key_rows.shape[0], head_count, HEAD_DIM)
    value_heads = value_rows.reshape(value_rows.shape[0], head_count, HEAD_DIM)
    scores = jnp.einsum(
        "qhd,khd->hqk", query_heads, key_heads, preferred_element_type=jnp.float32
    ) * HEAD_DIM ** (-0.5)
    scores = jnp.where(key_mask[None, None, :], scores, NEGATIVE)
    new_max = jnp.maximum(row_max, jnp.max(scores, axis=2))
    shrink = jnp.exp(row_max - new_max)
    weights = jnp.exp(scores - new_max[:, :, None])
    weight_sum = weight_sum * shrink + jnp.sum(weights, axis=2)
    mixed_sum = mixed_sum * shrink[:, :, None] + jnp.einsum(
        "hqk,khd->hqd",
        weights.astype(jnp.bfloat16),
        value_heads,
        preferred_element_type=jnp.float32,
    )
    return (new_max, weight_sum, mixed_sum)


def body(queries, keys, values, text_keys, text_values, prompt_lengths, frame_counts, out_weight):
    row_count = queries.shape[1]
    head_cols = queries.shape[2]
    head_count = head_cols // HEAD_DIM
    all_counts = gathered_copies(frame_counts, "seq", 0)
    query_heads = queries[0].reshape(row_count, head_count, HEAD_DIM)
    text_mask = jnp.arange(text_keys.shape[1], dtype=jnp.int32) < prompt_lengths[0]
    empty_state = (
        jnp.full((head_count, row_count), NEGATIVE, jnp.float32),
        jnp.zeros((head_count, row_count), jnp.float32),
        jnp.zeros((head_count, row_count, HEAD_DIM), jnp.float32),
    )
    text_state = attend_block(empty_state, text_keys[0], text_values[0], query_heads, text_mask)
    key_rows = lax.all_gather(keys[0], "seq", axis=0, tiled=True)
    value_rows = lax.all_gather(values[0], "seq", axis=0, tiled=True)
    positions = jnp.arange(key_rows.shape[0], dtype=jnp.int32)
    row_max, weight_sum, mixed_sum = attend_block(
        text_state, key_rows, value_rows, query_heads, frame_valid(positions, all_counts)
    )
    attended = (
        jnp.transpose(mixed_sum / weight_sum[:, :, None], (1, 0, 2))
        .reshape(row_count, head_cols)
        .astype(jnp.bfloat16)
    )
    projected = (
        lax.psum_scatter(
            lax.dot_general(
                out_weight, attended, (((0,), (1,)), ((), ())), preferred_element_type=jnp.float32
            ).astype(jnp.bfloat16),
            "tp",
            scatter_dimension=0,
            tiled=True,
        )
        .astype(jnp.float32)
        .T
    )
    branch = projected.astype(jnp.bfloat16)[None]
    paired = lax.all_to_all(branch, "cfg", split_axis=2, concat_axis=0, tiled=True)
    conditional = paired[0].astype(jnp.float32)
    unconditional = paired[1].astype(jnp.float32)
    guided = unconditional + GUIDANCE * (conditional - unconditional)
    token_weights = frame_valid(jnp.arange(row_count, dtype=jnp.int32), frame_counts).astype(
        jnp.float32
    )

    def local_sum(field_rows):
        return jnp.dot(token_weights, field_rows)

    guided_sum, guided_square, cond_sum, cond_square = together(
        (
            local_sum(guided),
            local_sum(guided * guided),
            local_sum(conditional),
            local_sum(conditional * conditional),
        ),
        "seq",
    )
    valid_total = jnp.sum(all_counts).astype(jnp.float32)
    guided_mean = guided_sum / valid_total
    guided_var = guided_square / valid_total - guided_mean * guided_mean
    cond_mean = cond_sum / valid_total
    cond_var = cond_square / valid_total - cond_mean * cond_mean
    std_ratio = jnp.sqrt((cond_var + 1.0) / (guided_var + 1.0))
    factor = RESCALE * std_ratio + (1.0 - RESCALE)
    return (guided_mean + (guided - guided_mean) * factor).astype(jnp.bfloat16)


def solution(mesh):
    placed = (
        P("cfg", "seq", "tp"),
        P("cfg", "seq", "tp"),
        P("cfg", "seq", "tp"),
        P("cfg", None, "tp"),
        P("cfg", None, "tp"),
        P("cfg"),
        P("seq"),
        P("tp", None),
    )
    return jax.shard_map(
        body, mesh=mesh, in_specs=placed, out_specs=P("seq", ("tp", "cfg")), check_vma=False
    )
```

profile of v0, /device:TPU:1, one launch (start us, length us, event | category | flops | bytes accessed | tf_op | source)
XLA Modules:
  0.0 327.0 jit_solution(5678599585954011462)
XLA Ops:
  6.5 0.0 all-gather.5.cloned.1.call-start
  6.5 0.7 all-gather.5.cloned.1.call-update
  7.3 0.0 all-gather.7.cloned.1.call-start
  7.3 0.7 all-gather.7.cloned.1.call-update
  8.7 0.6 broadcast_in_dim.95
  9.3 10.0 %all-to-all-start = ((s32[16,1,1]{2,1,0:T(1,128)}), s32[16,1,1]{2,1,0:T(1,128)S(1)}, u32[]{:S(2)}, u32[]{:S(2)}) async-start(s32[16,1,1]{2,1,0:T(1,128)} %broadcast_in_dim.95), calls=%async_computation | async-start | bytes 16384 | tf_op jit(solution)/shard_map/all_to_all | solution.py:21
  19.2 0.0 reduce-scatter.4.cloned.1.call-start
  19.3 1.3 copy.70
  21.2 1.3 copy.71
  22.6 3.2 fusion.7
  25.9 0.2 copy.74
  26.1 0.1 all-to-all-done
  26.2 1.0 fusion.62
  27.2 0.2 select_reduce_fusion
  27.4 48.6 %all-gather.5.cloned.1.call-done = bf16[1,7680,640]{2,1,0:T(8,128)(2,1)} async-done(((bf16[1,480,640]{2,1,0:T(8,128)(2,1)}), bf16[1,7680,640]{2,1,0:T(8,128)(2,1)}) %all-gather.5.cloned.1.call-update) | async-done | bytes 9830416 | tf_op jit(solution)/shard_map/all_gather | solution.py:87
  76.0 13.7 %copy.76 = bf16[1,7680,640]{1,2,0:T(8,128)(2,1)} copy(bf16[1,7680,640]{2,1,0:T(8,128)(2,1)} %all-gather.5.cloned.1.call-done) | data formatting | bytes 19660800 | tf_op jit(solution)/shard_map/all_gather | solution.py:87
  89.8 31.7 %fusion = (f32[5,480]{1,0:T(8,128)S(1)}, f32[5,480,7680]{2,1,0:T(8,128)}) fusion(pred[7680]{0:T(1024)(128)(4,1)S(1)} %fusion.41, bf16[480,5,128]{0,2,1:T(8,128)(2,1)S(1)} %bitcast.102, bf16[7680,5,128]{0,2,1:T(8,128)(2,1)} %bitcast.97), kind=kOutput, calls=%fused_computation.2 | convolution fusion | flops 4773885440 | bytes 84190080 | tf_op jit(solution)/shard_map/qhd,khd->hqk/dot_general | solution.py:57
  121.5 3.9 %fusion.8 = f32[5,480]{1,0:T(8,128)S(1)} fusion(f32[5,480,512]{2,1,0:T(8,128)} %get-tuple-element.17, f32[5,480]{1,0:T(8,128)S(1)} %get-tuple-element.11, pred[512]{0:T(512)(128)(4,1)S(1)} %iota_compare_fusion.2), kind=kLoop, calls=%fused_computation.12 | loop fusion | flops 4912800 | bytes 4934912 | tf_op jit(solution)/shard_map/reduce_sum | solution.py:64
  125.4 23.8 %fusion.1 = f32[5,480]{1,0:T(8,128)S(1)} fusion(f32[5,480,7680]{2,1,0:T(8,128)} %get-tuple-element.15, f32[5,480]{1,0:T(8,128)S(1)} %get-tuple-element.10, pred[7680]{0:T(1024)(128)(4,1)S(1)} %fusion.41), kind=kLoop, calls=%fused_computation.3 | loop fusion | flops 73725600 | bytes 73754880 | tf_op jit(solution)/shard_map/reduce_sum | solution.py:64
  149.3 1.7 fusion.28
  150.9 0.0 all-gather.7.cloned.1.call-done
  151.0 13.7 %copy.79 = bf16[1,7680,640]{1,2,0:T(8,128)(2,1)} copy(bf16[1,7680,640]{2,1,0:T(8,128)(2,1)} %all-gather.7.cloned.1.call-done) | data formatting | bytes 19660800 | tf_op jit(solution)/shard_map/all_gather | solution.py:88
  164.7 29.4 %fusion.34 = bf16[480,5,128]{2,0,1:T(8,128)(2,1)S(1)} fusion(f32[480,5,128]{2,0,1:T(8,128)S(1)} %fusion.28, bf16[7680,5,128]{0,2,1:T(8,128)(2,1)} %bitcast.100, f32[5,480,7680]{2,1,0:T(8,128)} %get-tuple-element.15, f32[5,480]{1,0:T(8,128)S(1)} %get-tuple-element.10, pred[7680]{0:T(1024)(128)(4,1)S(1)} %fusion.41, f32[480,5]{0,1:T(8,128)S(1)} %get-tuple-element.7), kind=kOutput, calls=%fused_computation.25 | convolution fusion | flops 4793241600 | bytes 85428480 | tf_op jit(solution)/shard_map/hqk,khd->hqd/dot_general | solution.py:65
  194.1 0.2 copy.81
  194.3 8.8 %fusion.6 = bf16[5120,480]{0,1:T(8,128)(2,1)} fusion(bf16[480,640]{0,1:T(8,128)(2,1)S(1)} %bitcast.116, bf16[640,5120]{1,0:T(8,128)(2,1)} %param.15), kind=kOutput, calls=%fused_computation.8 | convolution fusion | flops 3148185600 | bytes 12083200 | tf_op jit(solution)/shard_map/dot_general | solution.py:100
  203.2 7.8 %copy.91 = bf16[5120,480]{1,0:T(8,128)(2,1)} copy(bf16[5120,480]{0,1:T(8,128)(2,1)} %fusion.6) | data formatting | bytes 9830400
  211.0 0.0 reduce-scatter.4.cloned.1.call-update
  211.0 64.1 %reduce-scatter.4.cloned.1.call-done = bf16[640,480]{1,0:T(8,128)(2,1)} async-done(((bf16[5120,480]{1,0:T(8,128)(2,1)}), bf16[640,480]{1,0:T(8,128)(2,1)}) %reduce-scatter.4.cloned.1.call-update) | async-done | bytes 614416
  275.1 1.4 copy.92
  276.5 1.9 copy.82
  278.4 0.5 broadcast.122
  278.9 4.8 %reduce.13 = bf16[640,480]{1,0:T(8,128)(2,1)S(1)} reduce(bf16[640,1,480]{2,1,0:T(2,128)(2,1)S(1)} %bitcast.103, bf16[]{:T(256)} %broadcast.122), dimensions={1}, to_apply=%bitcast.78.reduce_sub_computation | reduce | bytes 1228802
  283.7 2.2 reshape.116
  285.9 3.7 %all-to-all-start.1 = ((bf16[2,2,76800]{2,1,0:T(2,128)(2,1)}), bf16[2,2,76800]{2,1,0:T(2,128)(2,1)S(1)}, u32[]{:S(2)}, u32[]{:S(2)}) async-start(bf16[2,2,76800]{2,1,0:T(2,128)(2,1)} %reshape.116), calls=%async_computation.1 | async-start | bytes 1228800 | tf_op jit(solution)/shard_map/all_to_all | solution.py:111
  289.7 9.5 %all-to-all-done.1 = bf16[2,2,76800]{2,1,0:T(2,128)(2,1)S(1)} async-done(((bf16[2,2,76800]{2,1,0:T(2,128)(2,1)}), bf16[2,2,76800]{2,1,0:T(2,128)(2,1)S(1)}, u32[]{:S(2)}, u32[]{:S(2)}) %all-to-all-start.1) | async-done | bytes 614432 | tf_op jit(solution)/shard_map/all_to_all | solution.py:111
  299.2 1.3 reshape.117
  300.5 0.2 copy.93
  300.6 0.2 convolution_reduce_fusion
  300.9 0.2 convolution_reduce_fusion.3
  301.1 0.3 convolution_reduce_fusion.1
  301.3 0.3 convolution_reduce_fusion.2
  301.6 0.1 concatenate.3
  301.7 0.7 broadcast_in_dim.102
  302.4 8.9 %all-to-all-start.2 = ((f32[16,1,1280]{2,1,0:T(1,128)}), f32[16,1,1280]{2,1,0:T(1,128)S(1)}, u32[]{:S(2)}, u32[]{:S(2)}) async-start(f32[16,1,1280]{2,1,0:T(1,128)} %broadcast_in_dim.102), calls=%async_computation.2 | async-start | bytes 163840 | tf_op jit(solution)/shard_map/all_to_all | solution.py:21
  311.9 7.5 %all-to-all-done.2 = f32[16,1,1280]{2,1,0:T(1,128)S(1)} async-done(((f32[16,1,1280]{2,1,0:T(1,128)}), f32[16,1,1280]{2,1,0:T(1,128)S(1)}, u32[]{:S(2)}, u32[]{:S(2)}) %all-to-all-start.2) | async-done | bytes 81952 | tf_op jit(solution)/shard_map/all_to_all | solution.py:21
  319.4 0.1 reduce_sum.58
  319.4 0.1 slice_divide_fusion
  319.5 0.9 add_convert_fusion
  (14 shorter events, 0.1 us)
Async XLA Ops:
  6.5 19.3 %copy-start = (bf16[1,512,640]{2,1,0:T(8,128)(2,1)S(1)}, bf16[1,512,640]{2,1,0:T(8,128)(2,1)}, u32[]{:S(2)}) copy-start(bf16[1,512,640]{2,1,0:T(8,128)(2,1)} %param.12) | copy-start | bytes 1966084
  6.5 69.5 %all-gather.5.cloned.1.call-start = ((), (), s32[]{:S(2)}) async-start(), calls=%async_computation.4 | async-start | bytes 10444800 | tf_op jit(solution)/shard_map/all_gather | solution.py:87
  7.3 143.7 %all-gather.7.cloned.1.call-start = ((), (), s32[]{:S(2)}) async-start(), calls=%async_computation.5 | async-start | bytes 10444800 | tf_op jit(solution)/shard_map/all_gather | solution.py:88
  9.3 16.9 %all-to-all-start = ((s32[16,1,1]{2,1,0:T(1,128)}), s32[16,1,1]{2,1,0:T(1,128)S(1)}, u32[]{:S(2)}, u32[]{:S(2)}) async-start(s32[16,1,1]{2,1,0:T(1,128)} %broadcast_in_dim.95), calls=%async_computation | async-start | bytes 16384 | tf_op jit(solution)/shard_map/all_to_all | solution.py:21
  19.2 255.8 %reduce-scatter.4.cloned.1.call-start = ((), (), s32[]{:S(2)}) async-start(), calls=%async_computation.6 | async-start | bytes 5898240
  121.5 27.8 %slice-start = ((s8[4915200]{0:T(1024)(128)(4,1)}), s8[4194304]{0:T(1024)(128)(4,1)S(1)}, s32[]{:S(2)}) async-start(s8[4915200]{0:T(1024)(128)(4,1)} %bitcast.98), calls=%async_computation.7 | async-start | bytes 8388608
  125.4 23.9 %slice-start.1 = ((s8[4915200]{0:T(1024)(128)(4,1)}), s8[720896]{0:T(1024)(128)(4,1)S(1)}, s32[]{:S(2)}) async-start(s8[4915200]{0:T(1024)(128)(4,1)} %bitcast.98), calls=%async_computation.8 | async-start | bytes 1441792
  285.9 13.3 %all-to-all-start.1 = ((bf16[2,2,76800]{2,1,0:T(2,128)(2,1)}), bf16[2,2,76800]{2,1,0:T(2,128)(2,1)S(1)}, u32[]{:S(2)}, u32[]{:S(2)}) async-start(bf16[2,2,76800]{2,1,0:T(2,128)(2,1)} %reshape.116), calls=%async_computation.1 | async-start | bytes 1228800 | tf_op jit(solution)/shard_map/all_to_all | solution.py:111
  302.4 17.0 %all-to-all-start.2 = ((f32[16,1,1280]{2,1,0:T(1,128)}), f32[16,1,1280]{2,1,0:T(1,128)S(1)}, u32[]{:S(2)}, u32[]{:S(2)}) async-start(f32[16,1,1280]{2,1,0:T(1,128)} %broadcast_in_dim.102), calls=%async_computation.2 | async-start | bytes 163840 | tf_op jit(solution)/shard_map/all_to_all | solution.py:21
Sparse Core Ops, SparseCore 0:
  9.2 66.8 all-gather.4
  77.9 61.1 all-gather.6
  211.1 63.8 reduce-scatter.3
where the time goes:
time: 328 us; the launch traced here: 327 us
  waiting for transfers between devices  131 us (40%)
  matrix products  75.7 us (23%)
  local copies, waits for them, and re-layouts  47.3 us (14%)
  other arithmetic  34.9 us (11%)
  starting transfers between devices  22.6 us (7%)
  between operations  15.2 us (5%)
    unnamed x4, waiting for transfers between devices  65.5 us
    all_gather x1, waiting for transfers between devices, body(): key_rows = lax.all_gather(keys[0], 'seq', axis=0, tiled=True)  48.6 us
    dot_general x2, matrix products, attend_block(): jnp.einsum('qhd,khd->hqk', query_heads, key_heads, preferred_element_type...  34.9 us
    dot_general x2, matrix products, attend_block(): jnp.einsum('hqk,khd->hqd', weights.astype(jnp.bfloat16), value_heads, pre...  31 us
    reduce_sum x2, other arithmetic, attend_block(): weight_sum = weight_sum * shrink + jnp.sum(weights, axis=2)  27.8 us
    all_to_all x2, starting transfers between devices, from_everyone(): lax.all_to_all(jnp.broadcast_to(value[None], (devices, *value.shape)), ax...  18.8 us
    unnamed x15, local copies, waits for them, and re-layouts  16.3 us
    all_gather x1, local copies, waits for them, and re-layouts, body(): value_rows = lax.all_gather(values[0], 'seq', axis=0, tiled=True)  13.7 us
  transfers between devices with their start and end apart: 6, of which 5 were waited for; matrix products, arithmetic and copies ran while one was open for 25% of the time, Pallas kernels for 0%

commit v1 on v0

--- a/solution.py
+++ b/solution.py
@@ -84,7 +84,11 @@
         jnp.zeros((head_count, row_count, HEAD_DIM), jnp.float32),
     )
     text_state = attend_block(empty_state, text_keys[0], text_values[0], query_heads, text_mask)
-    key_rows = lax.all_gather(keys[0], "seq", axis=0, tiled=True)
+    size = lax.axis_size("seq")
+    repeats = [size if d == 0 else 1 for d in range(keys[0].ndim)]
+    key_rows = lax.all_to_all(
+        jnp.tile(keys[0], repeats), "seq", split_axis=0, concat_axis=0, tiled=True
+    )
     value_rows = lax.all_gather(values[0], "seq", axis=0, tiled=True)
     positions = jnp.arange(key_rows.shape[0], dtype=jnp.int32)
     row_max, weight_sum, mixed_sum = attend_block(

time: 328 us -> 557 us (1.70)
  waiting for transfers between devices: 131 us -> 337 us
  blocking collectives: 0 us -> 16.8 us
  local copies, waits for them, and re-layouts: 47.3 us -> 58.5 us
    all_to_all x0 -> x1, waiting for transfers between devices: none -> 254 us  [body(): lax.all_to_all(jnp.tile(keys[0], repeats), 'seq', split_axis=0, concat_ax...]
    all_gather x1 -> x0, waiting for transfers between devices: 48.6 us -> none  [body(): key_rows = lax.all_gather(keys[0], 'seq', axis=0, tiled=True)]
    reshape x0 -> x1, local copies, waits for them, and re-layouts: none -> 22 us  [attend_block(): key_heads = key_rows.reshape(key_rows.shape[0], head_count, HEAD_DIM)]
    all_to_all x0 -> x1, blocking collectives: none -> 16.8 us  [from_everyone(): lax.all_to_all(jnp.broadcast_to(value[None], (devices, *value.shape)), ax...]
    all_gather x1 -> x0, local copies, waits for them, and re-layouts: 13.7 us -> none  [body(): key_rows = lax.all_gather(keys[0], 'seq', axis=0, tiled=True)]
    all_to_all x2 -> x1, starting transfers between devices: 18.8 us -> 8.92 us  [from_everyone(): lax.all_to_all(jnp.broadcast_to(value[None], (devices, *value.shape)), ax...]
    another operation x0 -> x1, local copies, waits for them, and re-layouts: none -> 5.6 us  [body(): jnp.tile(keys[0], repeats)]
    unnamed x15 -> x19, local copies, waits for them, and re-layouts: 16.3 us -> 14.2 us
  transfers between devices with their start and end apart: 6 -> 5, of which waited for: 5 -> 4; matrix products, arithmetic and copies ran while one was open for 25% -> 16% of each run, Pallas kernels for 0% -> 0%
where the time goes in v1:
time: 557 us; the launch traced here: 556 us
  waiting for transfers between devices  337 us (61%)
  matrix products  76.1 us (14%)
  local copies, waits for them, and re-layouts  58.5 us (11%)
  other arithmetic  34.2 us (6%)
  starting transfers between devices  18 us (3%)
  blocking collectives  16.8 us (3%)
  between operations  15.5 us (3%)
    all_to_all x1, waiting for transfers between devices, body(): lax.all_to_all(jnp.tile(keys[0], repeats), 'seq', split_axis=0, concat_ax...  254 us
    unnamed x3, waiting for transfers between devices  65.7 us
    dot_general x2, matrix products, attend_block(): jnp.einsum('qhd,khd->hqk', query_heads, key_heads, preferred_element_type...  35.4 us
    dot_general x2, matrix products, attend_block(): jnp.einsum('hqk,khd->hqd', weights.astype(jnp.bfloat16), value_heads, pre...  31 us
    reduce_sum x2, other arithmetic, attend_block(): weight_sum = weight_sum * shrink + jnp.sum(weights, axis=2)  27 us
    reshape x1, local copies, waits for them, and re-layouts, attend_block(): key_heads = key_rows.reshape(key_rows.shape[0], head_count, HEAD_DIM)  22 us
    all_to_all x1, blocking collectives, from_everyone(): lax.all_to_all(jnp.broadcast_to(value[None], (devices, *value.shape)), ax...  16.8 us
    unnamed x19, local copies, waits for them, and re-layouts  14.2 us
  transfers between devices with their start and end apart: 5, of which 4 were waited for; matrix products, arithmetic and copies ran while one was open for 16% of the time, Pallas kernels for 0%

profile of v1, /device:TPU:1, one launch (start us, length us, event | category | flops | bytes accessed | tf_op | source)
XLA Modules:
  0.0 555.7 jit_solution(11802831380905195080)
XLA Ops:
  7.2 16.8 %all_to_all.33 = s32[16,1,1]{2,1,0:T(1,128)S(1)} all-to-all(s32[16,1,1]{2,1,0:T(1,128)S(1)} %broadcast_in_dim.95), channel_id=1, replica_groups=mesh['cfg'=2,'seq'=16,'tp'=8] {'seq'}, dimensions={0} | all-to-all | bytes 128 | tf_op jit(solution)/shard_map/all_to_all | solution.py:21
  24.0 5.6 %tile.9 = bf16[16,480,640]{2,1,0:T(8,128)(2,1)} broadcast(bf16[480,640]{1,0:T(8,128)(2,1)} %bitcast.115), dimensions={1,2} | broadcast | bytes 10444800 | tf_op jit(solution)/shard_map/tile | solution.py:90
  29.6 5.3 all-to-all-start.1
  34.9 0.0 all-gather.3.cloned.1.call-start
  35.0 0.7 all-gather.3.cloned.1.call-update
  35.7 0.0 reduce-scatter.4.cloned.1.call-start
  35.7 0.0 copy-done.2
  35.7 0.3 copy.70
  36.6 0.0 copy-done
  36.6 0.3 copy.71
  36.9 0.3 copy.74
  37.2 3.1 fusion.9
  40.3 0.9 fusion.64
  41.3 0.2 select_reduce_fusion
  41.5 253.9 %all-to-all-done.1 = bf16[16,480,640]{2,1,0:T(8,128)(2,1)} async-done(((bf16[16,480,640]{2,1,0:T(8,128)(2,1)}), bf16[16,480,640]{2,1,0:T(8,128)(2,1)}, u32[]{:S(2)}, u32[]{:S(2)}) %all-to-all-start.1) | async-done | bytes 9830432 | tf_op jit(solution)/shard_map/all_to_all | solution.py:89
  295.3 22.0 %reshape.115 = bf16[7680,5,128]{2,1,0:T(8,128)(2,1)} reshape(bf16[16,480,640]{2,1,0:T(8,128)(2,1)} %all-to-all-done.1) | data formatting | bytes 19660800 | tf_op jit(solution)/shard_map/reshape | solution.py:55
  317.3 32.2 %fusion = (f32[5,480]{1,0:T(8,128)S(1)}, f32[5,480,7680]{2,1,0:T(8,128)}) fusion(pred[7680]{0:T(1024)(128)(4,1)S(1)} %fusion.43, bf16[480,5,128]{0,2,1:T(8,128)(2,1)S(1)} %bitcast.100, bf16[7680,5,128]{2,1,0:T(8,128)(2,1)} %reshape.115), kind=kOutput, calls=%fused_computation.2 | convolution fusion | flops 4773885440 | bytes 84190080 | tf_op jit(solution)/shard_map/qhd,khd->hqk/dot_general | solution.py:57
  349.6 3.8 fusion.10
  353.4 23.2 %fusion.1 = f32[5,480]{1,0:T(8,128)S(1)} fusion(f32[5,480,7680]{2,1,0:T(8,128)} %get-tuple-element.15, f32[5,480]{1,0:T(8,128)S(1)} %get-tuple-element.10, pred[7680]{0:T(1024)(128)(4,1)S(1)} %fusion.43), kind=kLoop, calls=%fused_computation.3 | loop fusion | flops 73725600 | bytes 73754880 | tf_op jit(solution)/shard_map/reduce_sum | solution.py:64
  376.7 1.7 fusion.30
  378.4 0.0 all-gather.3.cloned.1.call-done
  378.4 13.7 %copy.79 = bf16[1,7680,640]{1,2,0:T(8,128)(2,1)} copy(bf16[1,7680,640]{2,1,0:T(8,128)(2,1)} %all-gather.3.cloned.1.call-done) | data formatting | bytes 19660800 | tf_op jit(solution)/shard_map/all_gather | solution.py:92
  392.1 29.3 %fusion.36 = bf16[480,5,128]{2,0,1:T(8,128)(2,1)S(1)} fusion(f32[480,5,128]{2,0,1:T(8,128)S(1)} %fusion.30, bf16[7680,5,128]{0,2,1:T(8,128)(2,1)} %bitcast.98, f32[5,480,7680]{2,1,0:T(8,128)} %get-tuple-element.15, f32[5,480]{1,0:T(8,128)S(1)} %get-tuple-element.10, pred[7680]{0:T(1024)(128)(4,1)S(1)} %fusion.43, f32[480,5]{0,1:T(8,128)S(1)} %get-tuple-element.7), kind=kOutput, calls=%fused_computation.27 | convolution fusion | flops 4793241600 | bytes 85428480 | tf_op jit(solution)/shard_map/hqk,khd->hqd/dot_general | solution.py:65
  421.5 0.3 copy.81
  421.7 8.8 %fusion.8 = bf16[5120,480]{0,1:T(8,128)(2,1)} fusion(bf16[480,640]{0,1:T(8,128)(2,1)S(1)} %bitcast.114, bf16[640,5120]{1,0:T(8,128)(2,1)} %param.15), kind=kOutput, calls=%fused_computation.10 | convolution fusion | flops 3148185600 | bytes 12083200 | tf_op jit(solution)/shard_map/dot_general | solution.py:104
  430.5 7.8 %copy.94 = bf16[5120,480]{1,0:T(8,128)(2,1)} copy(bf16[5120,480]{0,1:T(8,128)(2,1)} %fusion.8) | data formatting | bytes 9830400
  438.4 0.0 reduce-scatter.4.cloned.1.call-update
  438.4 65.0 %reduce-scatter.4.cloned.1.call-done = bf16[640,480]{1,0:T(8,128)(2,1)} async-done(((bf16[5120,480]{1,0:T(8,128)(2,1)}), bf16[640,480]{1,0:T(8,128)(2,1)}) %reduce-scatter.4.cloned.1.call-update) | async-done | bytes 614416
  503.4 1.4 copy.95
  504.8 1.9 copy.82
  506.7 0.6 broadcast.124
  507.3 4.9 reduce.13
  512.2 2.2 reshape.123
  514.4 3.7 all-to-all-start.2
  518.1 9.5 %all-to-all-done.2 = bf16[2,2,76800]{2,1,0:T(2,128)(2,1)S(1)} async-done(((bf16[2,2,76800]{2,1,0:T(2,128)(2,1)}), bf16[2,2,76800]{2,1,0:T(2,128)(2,1)S(1)}, u32[]{:S(2)}, u32[]{:S(2)}) %all-to-all-start.2) | async-done | bytes 614432 | tf_op jit(solution)/shard_map/all_to_all | solution.py:115
  527.6 1.3 reshape.124
  528.9 0.2 copy.96
  529.1 0.2 convolution_reduce_fusion
  529.3 0.2 convolution_reduce_fusion.3
  529.5 0.3 convolution_reduce_fusion.1
  529.8 0.3 convolution_reduce_fusion.2
  530.0 0.1 concatenate.3
  530.1 0.7 broadcast_in_dim.102
  530.8 8.9 %all-to-all-start.3 = ((f32[16,1,1280]{2,1,0:T(1,128)}), f32[16,1,1280]{2,1,0:T(1,128)S(1)}, u32[]{:S(2)}, u32[]{:S(2)}) async-start(f32[16,1,1280]{2,1,0:T(1,128)} %broadcast_in_dim.102), calls=%async_computation.3 | async-start | bytes 163840 | tf_op jit(solution)/shard_map/all_to_all | solution.py:21
  540.3 7.5 %all-to-all-done.3 = f32[16,1,1280]{2,1,0:T(1,128)S(1)} async-done(((f32[16,1,1280]{2,1,0:T(1,128)}), f32[16,1,1280]{2,1,0:T(1,128)S(1)}, u32[]{:S(2)}, u32[]{:S(2)}) %all-to-all-start.3) | async-done | bytes 81952 | tf_op jit(solution)/shard_map/all_to_all | solution.py:21
  547.8 0.1 reduce_sum.58
  547.9 0.1 slice_divide_fusion
  548.0 0.9 add_convert_fusion
  (17 shorter events, 0.1 us)
Async XLA Ops:
  29.6 6.1 %copy-start.2 = (bf16[1,480,640]{2,1,0:T(8,128)(2,1)S(1)}, bf16[1,480,640]{2,1,0:T(8,128)(2,1)}, u32[]{:S(2)}) copy-start(bf16[1,480,640]{2,1,0:T(8,128)(2,1)} %param.8) | copy-start | bytes 1843204
  29.6 7.0 %copy-start = (bf16[1,512,640]{2,1,0:T(8,128)(2,1)S(1)}, bf16[1,512,640]{2,1,0:T(8,128)(2,1)}, u32[]{:S(2)}) copy-start(bf16[1,512,640]{2,1,0:T(8,128)(2,1)} %param.11) | copy-start | bytes 1966084
  29.6 7.3 %copy-start.1 = (bf16[1,512,640]{2,1,0:T(8,128)(2,1)S(1)}, bf16[1,512,640]{2,1,0:T(8,128)(2,1)}, u32[]{:S(2)}) copy-start(bf16[1,512,640]{2,1,0:T(8,128)(2,1)} %param.12) | copy-start | bytes 1966084
  29.6 265.7 %all-to-all-start.1 = ((bf16[16,480,640]{2,1,0:T(8,128)(2,1)}), bf16[16,480,640]{2,1,0:T(8,128)(2,1)}, u32[]{:S(2)}, u32[]{:S(2)}) async-start(bf16[16,480,640]{2,1,0:T(8,128)(2,1)} %tile.9), calls=%async_computation.1 | async-start | bytes 19660800 | tf_op jit(solution)/shard_map/all_to_all | solution.py:89
  34.9 343.4 %all-gather.3.cloned.1.call-start = ((), (), s32[]{:S(2)}) async-start(), calls=%async_computation.5 | async-start | bytes 10444800 | tf_op jit(solution)/shard_map/all_gather | solution.py:92
  35.7 467.7 %reduce-scatter.4.cloned.1.call-start = ((), (), s32[]{:S(2)}) async-start(), calls=%async_computation.6 | async-start | bytes 5898240
  349.6 27.1 %slice-start = ((s8[4915200]{0:T(1024)(128)(4,1)}), s8[4194304]{0:T(1024)(128)(4,1)S(1)}, s32[]{:S(2)}) async-start(s8[4915200]{0:T(1024)(128)(4,1)} %bitcast.96), calls=%async_computation.7 | async-start | bytes 8388608
  353.4 23.3 %slice-start.1 = ((s8[4915200]{0:T(1024)(128)(4,1)}), s8[720896]{0:T(1024)(128)(4,1)S(1)}, s32[]{:S(2)}) async-start(s8[4915200]{0:T(1024)(128)(4,1)} %bitcast.96), calls=%async_computation.8 | async-start | bytes 1441792
  514.4 13.2 %all-to-all-start.2 = ((bf16[2,2,76800]{2,1,0:T(2,128)(2,1)}), bf16[2,2,76800]{2,1,0:T(2,128)(2,1)S(1)}, u32[]{:S(2)}, u32[]{:S(2)}) async-start(bf16[2,2,76800]{2,1,0:T(2,128)(2,1)} %reshape.123), calls=%async_computation.2 | async-start | bytes 1228800 | tf_op jit(solution)/shard_map/all_to_all | solution.py:115
  530.8 17.0 %all-to-all-start.3 = ((f32[16,1,1280]{2,1,0:T(1,128)}), f32[16,1,1280]{2,1,0:T(1,128)S(1)}, u32[]{:S(2)}, u32[]{:S(2)}) async-start(f32[16,1,1280]{2,1,0:T(1,128)} %broadcast_in_dim.102), calls=%async_computation.3 | async-start | bytes 163840 | tf_op jit(solution)/shard_map/all_to_all | solution.py:21
Sparse Core Ops, SparseCore 0:
  37.6 196.1 all-gather.2
  438.5 64.8 reduce-scatter.3
